TPU v7x, 32 devices: a whole 2x2x4 slice. The times are simulated.
32 devices in a mesh: group: 2 (over y), view: 4 (over z), depth: 2 (over x), row: 2 (over core).
Axes of the slice: x: 2, y: 2, z: 4, core: 2. Of those that a mesh axis runs over, the one named last changes fastest.
Arguments:
- features: float32 [4, 32, 8, 512], P('view', None, ('group', 'row')), parts along dimension 2, may hold values from -6 to 6
- cotangent: float32 [8, 32, 8, 512], P('depth', 'view', ('group', 'row')), parts along dimension 2, may hold values from -6 to 6
- src_row: int32 [4, 8, 8, 512], P('view', 'depth', ('group', 'row')), parts along dimension 2, may hold values from -2 to 4, as said below
- src_col: int32 [4, 8, 8, 512], P('view', 'depth', ('group', 'row')), parts along dimension 2, may hold values from 0 to 510
- fractions: int32 [2, 4, 8, 8, 512], P(None, 'view', 'depth', ('group', 'row')), parts along dimension 3, may hold values from 0 to 256
Outputs:
- grad_features: float32 [4, 32, 8, 512], P('view', None, ('group', 'row'), 'depth'), parts along dimension 2
There are 2 independent parts, one for each index of `group`. A program takes and returns all parts, laid end to end along the dimension named above; each array names one. Nothing has to cross between parts.
Inputs may be any that keep to these rules, and one draw needn't show every extreme that they name: src_row[v, d, y, x] lies between y - 2 and y + 1.
All inputs are finite; a program needn't handle non-finite values.
Results may differ from a plain program's by a relative error of at most 0.0003.
Values sent between devices are 32-bit elements; how exact they have to be, the bound alone decides.
A program may use at most 64 MiB of HBM per device.

v0:
```python
import jax
import jax.numpy as jnp
from jax import lax
from jax.sharding import PartitionSpec as P

HALO = 2


def partner(shard, axis, apart):
    return lax.ppermute(shard, axis, [(i, i ^ 1 << apart) for i in range(lax.axis_size(axis))])


def with_halo(block, sides, width):
    for axis, dim in sides:
        count = lax.axis_size(axis)
        forward = [(i, i + 1) for i in range(count - 1)]
        backward = [(target, source) for source, target in forward]
        low = lax.ppermute(
            lax.slice_in_dim(block, block.shape[dim] - width, None, axis=dim), axis, forward
        )
        high = lax.ppermute(lax.slice_in_dim(block, 0, width, axis=dim), axis, backward)
        block = jnp.concatenate([low, block, high], axis=dim)
    return block


def sample(flattened, flat_index, frac_row, frac_col, width):

    def corner(shift_by):
        return jnp.take(flattened, flat_index + shift_by, axis=1)

    upper_mix = (1.0 - frac_col) * corner(0) + frac_col * corner(1)
    lower_mix = (1.0 - frac_col) * corner(width) + frac_col * corner(width + 1)
    mixed = (1.0 - frac_row) * upper_mix + frac_row * lower_mix
    return jnp.transpose(mixed, (1, 0, 2, 3))


def spread(grad_warp, flat_index, frac_row, frac_col, width, length):
    moved = jnp.transpose(grad_warp, (1, 0, 2, 3))
    channels = moved.shape[0]
    upper_part = (1.0 - frac_row) * moved
    lower_part = frac_row * moved
    result = jnp.zeros((channels, length), jnp.float32)
    result = result.at[:, flat_index].add((1.0 - frac_col) * upper_part)
    result = result.at[:, flat_index + 1].add(frac_col * upper_part)
    result = result.at[:, flat_index + width].add((1.0 - frac_col) * lower_part)
    result = result.at[:, flat_index + width + 1].add(frac_col * lower_part)
    return result


def fold_rims(grad_pad):
    upper_rim = grad_pad[:, :HALO]
    lower_rim = grad_pad[:, grad_pad.shape[1] - HALO :]
    interior = grad_pad[:, HALO : grad_pad.shape[1] - HALO]
    is_first = lax.axis_index("row") == 0
    outgoing = jnp.where(is_first, lower_rim, upper_rim)
    incoming = partner(outgoing, "row", 0)
    add_upper = jnp.where(is_first, 0.0, incoming)
    add_lower = jnp.where(is_first, incoming, 0.0)
    interior = interior.at[:, :HALO].add(add_upper)
    interior = interior.at[:, interior.shape[1] - HALO :].add(add_lower)
    return interior


def depth_reduce(partial_grad):
    return lax.psum_scatter(partial_grad, "depth", scatter_dimension=2, tiled=True)


def per_device(features, cotangent, src_row, src_col, fractions):
    channels = features.shape[1]
    row_count = features.shape[2]
    col_count = features.shape[3]
    padded = with_halo(features[0], (("row", 1),), HALO)
    padded_rows = row_count + 2 * HALO
    flattened = padded.reshape(channels, padded_rows * col_count)
    row_offset = lax.axis_index("row") * row_count
    flat_index = (src_row[0] - row_offset + HALO) * col_count + src_col[0]
    weights = fractions[:, 0].astype(jnp.float32) / 256.0
    warped = sample(flattened, flat_index, weights[0], weights[1], col_count)
    view_count = lax.axis_size("view") * features.shape[0]
    factor = 2.0 / view_count
    full_cotangent = lax.all_gather(cotangent, "view", axis=1, tiled=True)
    view_sum = lax.psum(warped, "view")
    average = view_sum / view_count
    grad_warp = factor * full_cotangent * (warped - average)
    spread_out = spread(
        grad_warp, flat_index, weights[0], weights[1], col_count, padded_rows * col_count
    )
    grad_pad = spread_out.reshape(channels, padded_rows, col_count)
    result = fold_rims(depth_reduce(grad_pad))
    return result[None]


def solution(mesh):
    in_specs = (
        P("view", None, ("group", "row"), None),
        P("depth", "view", ("group", "row"), None),
        P("view", "depth", ("group", "row"), None),
        P("view", "depth", ("group", "row"), None),
        P(None, "view", "depth", ("group", "row"), None),
    )
    out_specs = P("view", None, ("group", "row"), "depth")
    return jax.shard_map(
        per_device, mesh=mesh, in_specs=in_specs, out_specs=out_specs, check_vma=False
    )
```

profile of v0, /device:TPU:0, one launch (start us, length us, event | category | flops | bytes accessed | tf_op | source)
XLA Modules:
  0.0 254.8 jit_solution(4598418391159267502)
XLA Ops:
  6.5 2.4 collective-permute-start
  14.0 14.1 %gather_fusion = f32[4096,32]{1,0:T(8,128)} fusion(f32[32,3072]{0,1:T(8,128)S(1)} %bitcast.135, s32[4096]{0:T(1024)S(1)} %broadcast_clamp_fusion.3), kind=kCustom, calls=%fused_computation.clone | custom fusion | bytes 1064960 | tf_op jit(solution)/shard_map/jit(_take)/gather | solution.py:29
  28.1 1.9 copy.13
  30.0 14.1 %gather_fusion.1 = f32[4096,32]{1,0:T(8,128)} fusion(f32[32,3072]{0,1:T(8,128)S(1)} %bitcast.136, s32[4096]{0:T(1024)S(1)} %broadcast_clamp_fusion.2), kind=kCustom, calls=%fused_computation.1.clone | custom fusion | bytes 1064960 | tf_op jit(solution)/shard_map/jit(_take)/gather | solution.py:29
  44.1 1.9 copy.14
  46.0 14.1 %gather_fusion.2 = f32[4096,32]{1,0:T(8,128)} fusion(f32[32,3072]{0,1:T(8,128)S(1)} %bitcast.137, s32[4096]{0:T(1024)S(1)} %broadcast_clamp_fusion.1), kind=kCustom, calls=%fused_computation.2.clone | custom fusion | bytes 1064960 | tf_op jit(solution)/shard_map/jit(_take)/gather | solution.py:29
  60.1 1.9 copy.15
  62.0 14.1 %gather_fusion.3 = f32[4096,32]{1,0:T(8,128)} fusion(f32[32,3072]{0,1:T(8,128)S(1)} %bitcast.138, s32[4096]{0:T(1024)S(1)} %broadcast_clamp_fusion), kind=kCustom, calls=%fused_computation.3.clone | custom fusion | bytes 1064960 | tf_op jit(solution)/shard_map/jit(_take)/gather | solution.py:29
  76.0 1.9 copy.16
  78.0 1.7 fusion.5
  79.9 22.9 %all_gather.3 = f32[4,32,2,512]{3,2,1,0:T(2,128)S(1)} all-gather(f32[4,8,2,512]{3,2,1,0:T(2,128)S(1)} %copy-done), channel_id=1, replica_groups=mesh['group'=2,'view'=4,'depth'=2,'row'=2] {'view'}, dimensions={1}, use_global_device_ids=true | all-gather | bytes 655360 | tf_op jit(solution)/shard_map/all_gather | solution.py:81
  102.7 22.7 %all-reduce.2.cloned.1.call-done = f32[4,32,2,512]{3,2,1,0:T(2,128)} async-done(((f32[4,32,2,512]{3,2,1,0:T(2,128)}), f32[4,32,2,512]{3,2,1,0:T(2,128)}) %all-reduce.2.cloned.1.call-update) | async-done | bytes 524304 | tf_op jit(solution)/shard_map/psum | solution.py:82
  125.4 1.8 multiply_bitcast_fusion
  127.9 1.8 copy.26
  129.6 1.7 copy.27
  131.4 1.8 copy.28
  133.1 1.7 copy.29
  134.9 23.0 %scatter_custom_fusion = f32[32,3072]{0,1:T(8,128)S(1)} fusion(s32[4096]{0:T(1024)S(1)} %bitcast.158, f32[4096,32]{1,0:T(8,128)} %bitcast.147, f32[]{:T(128)} %constant.99.clone.1), kind=kCustom, calls=%fused_computation.8 | custom fusion | flops 131072 | bytes 393728 | tf_op jit(solution)/shard_map/scatter-add | solution.py:43
  157.9 23.3 %scatter_fusion = f32[32,3072]{0,1:T(8,128)S(1)} fusion(f32[32,3072]{0,1:T(8,128)S(1)} %scatter_custom_fusion, s32[4096]{0:T(1024)S(1)} %bitcast.153, f32[4096,32]{1,0:T(8,128)} %bitcast.142), kind=kCustom, calls=%fused_computation.5 | custom fusion | flops 131072 | bytes 1589248 | tf_op jit(solution)/shard_map/scatter-add | solution.py:44
  181.2 23.3 %scatter_fusion.1 = f32[32,3072]{0,1:T(8,128)S(1)} fusion(f32[32,3072]{0,1:T(8,128)S(1)} %scatter_fusion, s32[4096]{0:T(1024)S(1)} %bitcast.152, f32[4096,32]{1,0:T(8,128)} %bitcast.141), kind=kCustom, calls=%fused_computation.6 | custom fusion | flops 131072 | bytes 1589248 | tf_op jit(solution)/shard_map/scatter-add | solution.py:45
  204.4 23.4 %scatter_fusion.2 = f32[32,3072]{0,1:T(8,128)S(1)} fusion(f32[32,3072]{0,1:T(8,128)S(1)} %scatter_fusion.1, s32[4096]{0:T(1024)S(1)} %bitcast.151, f32[4096,32]{1,0:T(8,128)} %bitcast.140), kind=kCustom, calls=%fused_computation.7 | custom fusion | flops 131072 | bytes 1589248 | tf_op jit(solution)/shard_map/scatter-add | solution.py:46
  227.9 1.5 copy.25
  229.4 14.6 %reduce-scatter.2.cloned.1.call-done = f32[32,6,256]{2,1,0:T(8,128)} async-done(((f32[32,6,512]{2,1,0:T(8,128)}), f32[32,6,256]{2,1,0:T(8,128)}) %reduce-scatter.2.cloned.1.call-update) | async-done | bytes 196624 | tf_op jit(solution)/shard_map/reduce_scatter | solution.py:65
  246.4 1.6 fusion.9
  (33 shorter events, 8.1 us)
Async XLA Ops:
  6.5 118.9 %all-reduce.2.cloned.1.call-start = ((), (), s32[]{:S(2)}) async-start(), calls=%async_computation.1 | async-start | bytes 1048576 | tf_op jit(solution)/shard_map/psum | solution.py:82
  6.5 5.5 %collective-permute-start = (f32[32,2,512]{2,1,0:T(2,128)}, f32[32,2,512]{2,1,0:T(2,128)S(1)}, u32[]{:S(2)}, u32[]{:S(2)}) collective-permute-start(f32[32,2,512]{2,1,0:T(2,128)} %bitcast.148), channel_id=1, source_target_pairs={{0,1},{2,3},{4,5},{6,7},{8,9},{10,11},{12,13},{14,15},{16,17},{18,... | collective-permute-start | bytes 393224 | tf_op jit(solution)/shard_map/ppermute | solution.py:18
  8.9 3.5 %collective-permute-start.1 = (f32[32,2,512]{2,1,0:T(2,128)}, f32[32,2,512]{2,1,0:T(2,128)S(1)}, u32[]{:S(2)}, u32[]{:S(2)}) collective-permute-start(f32[32,2,512]{2,1,0:T(2,128)} %bitcast.149), channel_id=1, source_target_pairs={{1,0},{3,2},{5,4},{7,6},{9,8},{11,10},{13,12},{15,14},{17,16},{19,... | collective-permute-start | bytes 393224 | tf_op jit(solution)/shard_map/ppermute | solution.py:21
  77.9 1.9 copy-start
  79.7 164.2 %reduce-scatter.2.cloned.1.call-start = ((), (), s32[]{:S(2)}) async-start(), calls=%async_computation.2 | async-start | bytes 786432 | tf_op jit(solution)/shard_map/reduce_scatter | solution.py:65
  245.0 1.3 collective-permute-start.2
Sparse Core Ops, SparseCore 0:
  79.8 45.5 all-reduce.1
  229.5 14.4 reduce-scatter.1
where the time goes:
time: 255 us
  other arithmetic  103 us (40%)
  local copies, waits for them, and re-layouts  72.9 us (29%)
  waiting for transfers between devices  38.9 us (15%)
  blocking collectives  22.9 us (9%)
  between operations  13.7 us (5%)
  starting transfers between devices  3.8 us (1%)
    gather x8, local copies, waits for them, and re-layouts, corner(): return jnp.take(flattened, flat_index + shift_by, axis=1)  63.9 us
    scatter-add x1, other arithmetic, spread(): result = result.at[:, flat_index + width + 1].add(frac_col * lower_part)  23.4 us
    scatter-add x1, other arithmetic, spread(): result = result.at[:, flat_index + 1].add(frac_col * upper_part)  23.3 us
    scatter-add x1, other arithmetic, spread(): result = result.at[:, flat_index + width].add((1.0 - frac_col) * lower_part)  23.3 us
    scatter-add x1, other arithmetic, spread(): result = result.at[:, flat_index].add((1.0 - frac_col) * upper_part)  23 us
    all_gather x1, blocking collectives, per_device(): full_cotangent = lax.all_gather(cotangent, 'view', axis=1, tiled=True)  22.9 us
    psum x1, waiting for transfers between devices, per_device(): view_sum = lax.psum(warped, 'view')  22.7 us
    reduce_scatter x1, waiting for transfers between devices, depth_reduce(): lax.psum_scatter(partial_grad, 'depth', scatter_dimension=2, tiled=True)  14.6 us
  transfers between devices with their start and end apart: 5, of which 4 were waited for; matrix products, arithmetic and copies ran while one was open for 1% of the time, Pallas kernels for 0%

commit v1 on v0

--- a/solution.py
+++ b/solution.py
@@ -78,7 +78,8 @@
     warped = sample(flattened, flat_index, weights[0], weights[1], col_count)
     view_count = lax.axis_size("view") * features.shape[0]
     factor = 2.0 / view_count
-    full_cotangent = lax.all_gather(cotangent, "view", axis=1, tiled=True)
+    blocks = lax.all_gather(cotangent, "view")
+    full_cotangent = jnp.concatenate(blocks, axis=1)
     view_sum = lax.psum(warped, "view")
     average = view_sum / view_count
     grad_warp = factor * full_cotangent * (warped - average)

time: 255 us -> 256 us (level)
  no operation moved by 1% of the time
where the time goes in v1:
time: 256 us; the launch traced here: 255 us
  other arithmetic  101 us (39%)
  local copies, waits for them, and re-layouts  75.1 us (29%)
  waiting for transfers between devices  38.8 us (15%)
  blocking collectives  22.9 us (9%)
  between operations  13.7 us (5%)
  starting transfers between devices  3.8 us (1%)
    gather x8, local copies, waits for them, and re-layouts, corner(): return jnp.take(flattened, flat_index + shift_by, axis=1)  65.3 us
    scatter-add x1, other arithmetic, spread(): result = result.at[:, flat_index + width + 1].add(frac_col * lower_part)  23.4 us
    scatter-add x1, other arithmetic, spread(): result = result.at[:, flat_index + 1].add(frac_col * upper_part)  23.3 us
    scatter-add x1, other arithmetic, spread(): result = result.at[:, flat_index + width].add((1.0 - frac_col) * lower_part)  23.3 us
    scatter-add x1, other arithmetic, spread(): result = result.at[:, flat_index].add((1.0 - frac_col) * upper_part)  23 us
    all_gather x1, blocking collectives, per_device(): blocks = lax.all_gather(cotangent, 'view')  22.9 us
    psum x1, waiting for transfers between devices, per_device(): view_sum = lax.psum(warped, 'view')  22.6 us
    reduce_scatter x1, waiting for transfers between devices, depth_reduce(): lax.psum_scatter(partial_grad, 'depth', scatter_dimension=2, tiled=True)  14.6 us
  transfers between devices with their start and end apart: 5, of which 4 were waited for; matrix products, arithmetic and copies ran while one was open for 1% of the time, Pallas kernels for 0%

profile of v1, /device:TPU:0, one launch (start us, length us, event | category | flops | bytes accessed | tf_op | source)
XLA Modules:
  0.0 255.4 jit_solution(15244349749900589649)
XLA Ops:
  6.5 2.4 collective-permute-start
  8.9 1.3 collective-permute-start.1
  14.0 14.2 %gather_fusion = f32[4096,32]{1,0:T(8,128)} fusion(f32[32,3072]{0,1:T(8,128)S(1)} %bitcast.141, s32[4096]{0:T(1024)S(1)} %broadcast_clamp_fusion.3), kind=kCustom, calls=%fused_computation.clone | custom fusion | bytes 1064960 | tf_op jit(solution)/shard_map/jit(_take)/gather | solution.py:29
  28.1 2.2 copy.34
  30.3 14.2 %gather_fusion.1 = f32[4096,32]{1,0:T(8,128)} fusion(f32[32,3072]{0,1:T(8,128)S(1)} %bitcast.142, s32[4096]{0:T(1024)S(1)} %broadcast_clamp_fusion.2), kind=kCustom, calls=%fused_computation.1.clone | custom fusion | bytes 1064960 | tf_op jit(solution)/shard_map/jit(_take)/gather | solution.py:29
  44.5 2.2 copy.35
  46.6 14.2 %gather_fusion.2 = f32[4096,32]{1,0:T(8,128)} fusion(f32[32,3072]{0,1:T(8,128)S(1)} %bitcast.143, s32[4096]{0:T(1024)S(1)} %broadcast_clamp_fusion.1), kind=kCustom, calls=%fused_computation.2.clone | custom fusion | bytes 1064960 | tf_op jit(solution)/shard_map/jit(_take)/gather | solution.py:29
  60.8 2.2 copy.36
  62.9 14.2 %gather_fusion.3 = f32[4096,32]{1,0:T(8,128)} fusion(f32[32,3072]{0,1:T(8,128)S(1)} %bitcast.144, s32[4096]{0:T(1024)S(1)} %broadcast_clamp_fusion), kind=kCustom, calls=%fused_computation.3.clone | custom fusion | bytes 1064960 | tf_op jit(solution)/shard_map/jit(_take)/gather | solution.py:29
  77.1 2.2 copy.37
  80.6 22.9 %all-gather = f32[16,8,2,512]{3,1,2,0:T(8,128)S(1)} all-gather(f32[4,8,2,512]{3,1,2,0:T(8,128)S(1)} %copy.31), channel_id=2, replica_groups=mesh['group'=2,'view'=4,'depth'=2,'row'=2] {'view'}, dimensions={0}, use_global_device_ids=true | all-gather | bytes 655360 | tf_op jit(solution)/shard_map/all_gather | solution.py:81
  103.5 22.6 %all-reduce.2.cloned.1.call-done = f32[4,32,2,512]{3,1,2,0:T(8,128)} async-done(((f32[4,32,2,512]{3,1,2,0:T(8,128)}), f32[4,32,2,512]{3,1,2,0:T(8,128)}) %all-reduce.2.cloned.1.call-update) | async-done | bytes 524304 | tf_op jit(solution)/shard_map/psum | solution.py:83
  127.6 2.0 copy.47
  129.6 1.9 copy.48
  131.5 1.9 copy.49
  133.4 1.9 copy.50
  135.4 23.0 %scatter_custom_fusion = f32[32,3072]{0,1:T(8,128)S(1)} fusion(s32[4096]{0:T(1024)S(1)} %bitcast.165, f32[4096,32]{1,0:T(8,128)} %bitcast.153, f32[]{:T(128)} %constant.99.clone.1), kind=kCustom, calls=%fused_computation.8 | custom fusion | flops 131072 | bytes 393728 | tf_op jit(solution)/shard_map/scatter-add | solution.py:43
  158.4 23.3 %scatter_fusion = f32[32,3072]{0,1:T(8,128)S(1)} fusion(f32[32,3072]{0,1:T(8,128)S(1)} %scatter_custom_fusion, s32[4096]{0:T(1024)S(1)} %bitcast.160, f32[4096,32]{1,0:T(8,128)} %bitcast.148), kind=kCustom, calls=%fused_computation.5 | custom fusion | flops 131072 | bytes 1589248 | tf_op jit(solution)/shard_map/scatter-add | solution.py:44
  181.7 23.3 %scatter_fusion.1 = f32[32,3072]{0,1:T(8,128)S(1)} fusion(f32[32,3072]{0,1:T(8,128)S(1)} %scatter_fusion, s32[4096]{0:T(1024)S(1)} %bitcast.159, f32[4096,32]{1,0:T(8,128)} %bitcast.147), kind=kCustom, calls=%fused_computation.6 | custom fusion | flops 131072 | bytes 1589248 | tf_op jit(solution)/shard_map/scatter-add | solution.py:45
  204.9 23.4 %scatter_fusion.2 = f32[32,3072]{0,1:T(8,128)S(1)} fusion(f32[32,3072]{0,1:T(8,128)S(1)} %scatter_fusion.1, s32[4096]{0:T(1024)S(1)} %bitcast.158, f32[4096,32]{1,0:T(8,128)} %bitcast.146), kind=kCustom, calls=%fused_computation.7 | custom fusion | flops 131072 | bytes 1589248 | tf_op jit(solution)/shard_map/scatter-add | solution.py:46
  228.4 1.4 copy.46
  229.9 14.6 %reduce-scatter.2.cloned.1.call-done = f32[32,6,256]{2,1,0:T(8,128)} async-done(((f32[32,6,512]{2,1,0:T(8,128)}), f32[32,6,256]{2,1,0:T(8,128)}) %reduce-scatter.2.cloned.1.call-update) | async-done | bytes 196624 | tf_op jit(solution)/shard_map/reduce_scatter | solution.py:65
  245.6 1.2 collective-permute-done.2
  246.9 1.6 fusion.9
  (37 shorter events, 7.6 us)
Async XLA Ops:
  6.5 119.6 %all-reduce.2.cloned.1.call-start = ((), (), s32[]{:S(2)}) async-start(), calls=%async_computation.1 | async-start | bytes 1048576 | tf_op jit(solution)/shard_map/psum | solution.py:83
  6.5 5.5 %collective-permute-start = (f32[32,2,512]{2,1,0:T(2,128)}, f32[32,2,512]{2,1,0:T(2,128)S(1)}, u32[]{:S(2)}, u32[]{:S(2)}) collective-permute-start(f32[32,2,512]{2,1,0:T(2,128)} %bitcast.155), channel_id=1, source_target_pairs={{0,1},{2,3},{4,5},{6,7},{8,9},{10,11},{12,13},{14,15},{16,17},{18,... | collective-permute-start | bytes 393224 | tf_op jit(solution)/shard_map/ppermute | solution.py:18
  8.9 3.5 %collective-permute-start.1 = (f32[32,2,512]{2,1,0:T(2,128)}, f32[32,2,512]{2,1,0:T(2,128)S(1)}, u32[]{:S(2)}, u32[]{:S(2)}) collective-permute-start(f32[32,2,512]{2,1,0:T(2,128)} %bitcast.156), channel_id=1, source_target_pairs={{1,0},{3,2},{5,4},{7,6},{9,8},{11,10},{13,12},{15,14},{17,16},{19,... | collective-permute-start | bytes 393224 | tf_op jit(solution)/shard_map/ppermute | solution.py:21
  79.3 1.3 copy-start.1
  80.4 45.7 %copy-start = (f32[4,32,2,512]{3,1,2,0:T(8,128)S(1)}, f32[4,32,2,512]{3,1,2,0:T(8,128)}, u32[]{:S(2)}) copy-start(f32[4,32,2,512]{3,1,2,0:T(8,128)} %fusion.5) | copy-start | bytes 1572868
  80.4 164.0 %reduce-scatter.2.cloned.1.call-start = ((), (), s32[]{:S(2)}) async-start(), calls=%async_computation.2 | async-start | bytes 786432 | tf_op jit(solution)/shard_map/reduce_scatter | solution.py:65
  245.6 1.3 collective-permute-start.2
Sparse Core Ops, SparseCore 0:
  80.6 45.5 all-reduce.1
  230.0 14.4 reduce-scatter.1
